TPU v7x, 32 devices: a whole 2x2x4 slice. The times are simulated.
32 devices in a mesh: grp: 4 (over x, core), tile: 8 (over z, y).
Axes of the slice: x: 2, y: 2, z: 4, core: 2. Of those that a mesh axis runs over, the one named last changes fastest.
Arguments:
- flow_state: float32 [4, 4, 32, 2048], P('grp', None, 'tile'), may hold values from -6 to 6
- line_owner: int32 [8192, 1], replicated, may hold values from 0 to 7; in each aligned block of 8192 rows (0 to 8191, 8192 to 16383, ...) at most 2048 rows name the same one
Outputs:
- record: float32 [4, 8, 32, 2048], P('grp', 'tile')
Inputs may be any that keep to these rules, and one draw needn't show every extreme that they name: `line_owner`: no pencil owns more than 2048 lines, some pencil owns exactly 2048, and every pencil owns at least one line.
All inputs are finite; a program needn't handle non-finite values.
Results may differ from a plain program's by a relative error of at most 0.00002.
Values sent between devices are 32-bit elements; how exact they have to be, the bound alone decides.
A program may use at most 64 MiB of HBM per device.

v0:
```python
import jax
import jax.numpy as jnp
from jax import lax
from jax.sharding import PartitionSpec as P

time_step = 0.2
viscosity = 0.05
stencil_reach = 4
first_coeffs = (0.8, -0.2, 4.0 / 105.0, -1.0 / 280.0)
second_center = -205.0 / 72.0
second_coeffs = (1.6, -0.2, 8.0 / 315.0, -1.0 / 560.0)
lift_alpha = -1.586134342059924
lift_beta = -0.052980118572961
lift_gamma = 0.882911075530934
lift_delta = 0.443506852043971
lift_scale = 1.149604398860241


def with_halo(cells, sides, width):
    for axis, dim in sides:
        count = lax.axis_size(axis)
        head = lax.slice_in_dim(cells, 0, width, axis=dim)
        tail = lax.slice_in_dim(cells, cells.shape[dim] - width, cells.shape[dim], axis=dim)
        cells = jnp.concatenate(
            [
                lax.ppermute(tail, axis, [(i, (i + 1) % count) for i in range(count)]),
                cells,
                lax.ppermute(head, axis, [((i + 1) % count, i) for i in range(count)]),
            ],
            axis=dim,
        )
    return cells


def first_rolled(field_now, along_axis):
    running = jnp.zeros_like(field_now)
    for offset in range(4):
        forward = jnp.roll(field_now, -(offset + 1), along_axis)
        behind = jnp.roll(field_now, offset + 1, along_axis)
        running = running + first_coeffs[offset] * (forward - behind)
    return running


def second_rolled(field_now, along_axis):
    running = second_center * field_now
    for offset in range(4):
        forward = jnp.roll(field_now, -(offset + 1), along_axis)
        behind = jnp.roll(field_now, offset + 1, along_axis)
        running = running + second_coeffs[offset] * (forward + behind)
    return running


def first_padded(padded, rows_here):
    running = jnp.zeros((padded.shape[0], rows_here, padded.shape[2]), jnp.float32)
    for offset in range(4):
        forward = padded[:, stencil_reach + offset + 1 : stencil_reach + offset + 1 + rows_here]
        behind = padded[:, stencil_reach - offset - 1 : stencil_reach - offset - 1 + rows_here]
        running = running + first_coeffs[offset] * (forward - behind)
    return running


def second_padded(padded, rows_here):
    running = second_center * padded[:, stencil_reach : stencil_reach + rows_here]
    for offset in range(4):
        forward = padded[:, stencil_reach + offset + 1 : stencil_reach + offset + 1 + rows_here]
        behind = padded[:, stencil_reach - offset - 1 : stencil_reach - offset - 1 + rows_here]
        running = running + second_coeffs[offset] * (forward + behind)
    return running


def local_tendency(velocity, own_padded, press_padded, group_index):
    rows_here = velocity.shape[2]
    own_field = own_padded[:, stencil_reach : stencil_reach + rows_here]
    press_field = press_padded[:, stencil_reach : stencil_reach + rows_here]
    advect = (
        velocity[0] * first_padded(own_padded, rows_here)
        + velocity[1] * first_rolled(own_field, 2)
        + velocity[2] * first_rolled(own_field, 0)
    )
    laplace = (
        second_padded(own_padded, rows_here)
        + second_rolled(own_field, 2)
        + second_rolled(own_field, 0)
    )
    pressure_grad = lax.switch(
        jnp.minimum(group_index, 3),
        [
            lambda: first_padded(press_padded, rows_here),
            lambda: first_rolled(press_field, 2),
            lambda: first_rolled(press_field, 0),
            lambda: jnp.zeros_like(own_field),
        ],
    )
    tendency = -advect - pressure_grad + viscosity * laplace
    return jnp.where(group_index < 3, tendency, 0.0)


def section_tendency(current, group_index):
    fields = lax.all_gather(current, "grp", axis=0, tiled=True)
    stacked = jnp.concatenate([current, fields[3:4]], 0)
    padded = with_halo(stacked, (("tile", 2),), stencil_reach)
    return local_tendency(fields[:3], padded[0], padded[1], group_index)


def lift_axis(signal, along_axis):
    length = signal.shape[along_axis]
    even_part = lax.slice_in_dim(signal, 0, length, 2, along_axis)
    odd_part = lax.slice_in_dim(signal, 1, length, 2, along_axis)
    odd_part = odd_part + lift_alpha * (even_part + jnp.roll(even_part, -1, along_axis))
    even_part = even_part + lift_beta * (odd_part + jnp.roll(odd_part, 1, along_axis))
    odd_part = odd_part + lift_gamma * (even_part + jnp.roll(even_part, -1, along_axis))
    even_part = even_part + lift_delta * (odd_part + jnp.roll(odd_part, 1, along_axis))
    return jnp.concatenate([even_part * lift_scale, odd_part / lift_scale], along_axis)


def line_slots(line_owner, pencils, capacity):
    owners = line_owner[:, 0]
    sorted_lines = jnp.argsort(owners, stable=True)
    sorted_owner = owners[sorted_lines]
    targets = jnp.arange(pencils, dtype=jnp.int32)
    starts = jnp.searchsorted(sorted_owner, targets, side="left")
    ends_at = jnp.searchsorted(sorted_owner, targets, side="right")
    counts = ends_at - starts
    slot_index = jnp.arange(capacity, dtype=jnp.int32)
    position = jnp.minimum(starts[:, None] + slot_index[None, :], owners.shape[0] - 1)
    chosen = sorted_lines[position]
    usable = slot_index[None, :] < counts[:, None]
    return (chosen, usable)


def body(flow_state, line_owner):
    group_index = lax.axis_index("grp")
    middle = flow_state + time_step * section_tendency(flow_state, group_index)[None]
    finished = 0.5 * (flow_state + middle + time_step * section_tendency(middle, group_index)[None])
    coeffs = lift_axis(lift_axis(finished[0], 2), 0)
    planes, rows_here, columns = coeffs.shape
    line_table = jnp.transpose(coeffs, (1, 0, 2)).reshape(rows_here, planes * columns)
    pencils = lax.axis_size("tile")
    capacity = 2 * planes * columns // pencils
    chosen, usable = line_slots(line_owner, pencils, capacity)
    outgoing = jnp.take(line_table, chosen.reshape(-1), axis=1)
    outgoing = jnp.where(usable.reshape(-1)[None, :], outgoing, 0.0)
    received = lax.all_to_all(outgoing, "tile", split_axis=1, concat_axis=0, tiled=True)
    record = lift_axis(received, 0)
    all_coeffs = lax.all_gather(record[None], "grp", axis=0, tiled=True)
    energy = (
        all_coeffs[0] * all_coeffs[0]
        + all_coeffs[1] * all_coeffs[1]
        + all_coeffs[2] * all_coeffs[2]
    )
    return jnp.where(group_index == 3, energy, record)[None, None]


def solution(mesh):
    in_specs = (P("grp", None, "tile", None), P())
    out_specs = P("grp", "tile", None, None)
    return jax.shard_map(body, mesh=mesh, in_specs=in_specs, out_specs=out_specs, check_vma=False)
```

profile of v0, /device:TPU:0, one launch (start us, length us, event | category | flops | bytes accessed | tf_op | source)
XLA Modules:
  0.0 322.8 jit_solution(14009630170293777985)
XLA Ops:
  6.5 9.0 %all_gather.9 = f32[4,4,4,2048]{3,2,1,0:T(4,128)S(1)} all-gather(f32[1,4,4,2048]{3,2,1,0:T(4,128)} %param.14), channel_id=1, replica_groups=mesh['grp'=4,'tile'=8] {'grp'}, dimensions={0}, use_global_device_ids=true | all-gather | bytes 655360 | tf_op jit(solution)/shard_map/all_gather | solution.py:99
  15.5 1.0 pad_maximum_fusion.6
  16.5 4.6 %collective-permute-start.1 = (f32[2,4,4,2048]{3,2,1,0:T(4,128)S(1)}, f32[2,4,4,2048]{3,2,1,0:T(4,128)S(1)}, u32[]{:S(2)}, u32[]{:S(2)}) collective-permute-start(f32[2,4,4,2048]{3,2,1,0:T(4,128)S(1)} %pad_maximum_fusion.6), channel_id=1, source_target_pairs={{1,0},{2,1},{3,2},{4,3},{5,4},{6,5},{7,6},{0,7},{9,8},{10,9},{11,1... | collective-permute-start | bytes 786440 | tf_op jit(solution)/shard_map/ppermute | solution.py:28
  21.1 7.5 %sort.17 = (s32[8192]{0:T(1024)}, s32[8192]{0:T(1024)S(1)}) sort(s32[8192]{0:T(1024)} %bitcast.127, s32[8192]{0:T(1024)S(1)} %iota.16), dimensions={0}, to_apply=%region_0.1 | sort | flops 106496 | bytes 131072 | tf_op jit(solution)/shard_map/jit(argsort)/sort | solution.py:118
  28.7 45.5 %gather_fusion.2 = s32[8192]{0:T(1024)S(1)} fusion(s32[8192]{0:T(1024)S(1)} %bitcast.128, s32[8192]{0:T(1024)S(1)} %fusion.108), kind=kCustom, calls=%fused_computation.2 | custom fusion | bytes 98304 | tf_op jit(solution)/shard_map/gather | solution.py:119
  74.2 9.7 %while.49 = (s32[]{:T(128)}, u32[8]{0:T(128)S(1)}, u32[8]{0:T(128)S(1)}, s32[8192]{0:T(1024)S(1)}, s32[]{:T(128)}, /*index=5*/s32[]{:T(128)}, s32[]{}) while((s32[]{:T(128)}, u32[8]{0:T(128)S(1)}, u32[8]{0:T(128)S(1)}, s32[8192]{0:T(1024)S(1)}, s32[]{:T(128)}, /*index=5*/s32[]{:T(128)}, s32[]{}) %tuple.139), condition=%wide.region_4.5_spmd.clone, body=%wide.region_3.4_spmd.clone.sunk | while | flops 1132 | bytes 4580 | solution.py:121
  74.3 0.6 gather_fusion.1
  74.9 0.6 gather_fusion.1
  75.6 0.6 gather_fusion.1
  76.3 0.6 gather_fusion.1
  77.0 0.6 gather_fusion.1
  77.7 0.6 gather_fusion.1
  78.4 0.6 gather_fusion.1
  79.1 0.6 gather_fusion.1
  79.8 0.6 gather_fusion.1
  80.5 0.6 gather_fusion.1
  81.2 0.6 gather_fusion.1
  81.9 0.6 gather_fusion.1
  82.6 0.6 gather_fusion.1
  83.3 0.6 gather_fusion.1
  83.9 9.7 %while.48 = (s32[]{:T(128)}, u32[8]{0:T(128)S(1)}, u32[8]{0:T(128)S(1)}, s32[8192]{0:T(1024)S(1)}, s32[]{:T(128)}, /*index=5*/s32[]{:T(128)}, s32[]{}) while((s32[]{:T(128)}, u32[8]{0:T(128)S(1)}, u32[8]{0:T(128)S(1)}, s32[8192]{0:T(1024)S(1)}, s32[]{:T(128)}, /*index=5*/s32[]{:T(128)}, s32[]{}) %tuple.155), condition=%wide.region_2.3_spmd.clone, body=%wide.region_1.2_spmd.clone.sunk | while | flops 1132 | bytes 4580 | solution.py:122
  84.0 0.6 gather_fusion
  84.7 0.6 gather_fusion
  85.4 0.6 gather_fusion
  86.1 0.6 gather_fusion
  86.7 0.6 gather_fusion
  87.4 0.6 gather_fusion
  88.1 0.6 gather_fusion
  88.8 0.6 gather_fusion
  89.5 0.6 gather_fusion
  90.2 0.6 gather_fusion
  90.9 0.6 gather_fusion
  91.6 0.6 gather_fusion
  92.3 0.6 gather_fusion
  93.0 0.6 gather_fusion
  93.8 90.5 %gather_fusion.3 = s32[16384]{0:T(1024)S(1)} fusion(s32[8192]{0:T(1024)S(1)} %get-tuple-element.168, s32[16384]{0:T(1024)S(1)} %broadcast_clamp_fusion.1), kind=kCustom, calls=%fused_computation.3 | custom fusion | bytes 196608 | tf_op jit(solution)/shard_map/gather | solution.py:126
  184.5 0.2 pad_maximum_fusion.4
  185.2 0.1 fusion.148
  185.3 0.1 fusion.146
  185.4 0.1 fusion.150
  185.6 0.1 fusion.152
  185.7 0.3 conditional.2
  185.8 0.2 fusion.5
  186.0 1.0 fusion.70
  187.0 7.8 %all_gather.10 = f32[4,4,4,2048]{3,2,1,0:T(4,128)S(1)} all-gather(f32[1,4,4,2048]{3,2,1,0:T(4,128)S(1)} %fusion.70), channel_id=1, replica_groups=mesh['grp'=4,'tile'=8] {'grp'}, dimensions={0}, use_global_device_ids=true | all-gather | bytes 655360 | tf_op jit(solution)/shard_map/all_gather | solution.py:99
  194.9 4.7 %collective-permute-start.3 = (f32[2,4,4,2048]{3,2,1,0:T(4,128)S(1)}, f32[2,4,4,2048]{3,2,1,0:T(4,128)S(1)}, u32[]{:S(2)}, u32[]{:S(2)}) collective-permute-start(f32[2,4,4,2048]{3,2,1,0:T(4,128)S(1)} %pad_maximum_fusion.7), channel_id=1, source_target_pairs={{1,0},{2,1},{3,2},{4,3},{5,4},{6,5},{7,6},{0,7},{9,8},{10,9},{11,1... | collective-permute-start | bytes 786440 | tf_op jit(solution)/shard_map/ppermute | solution.py:28
  199.7 6.0 %collective-permute-done.3 = f32[2,4,4,2048]{3,2,1,0:T(4,128)S(1)} collective-permute-done((f32[2,4,4,2048]{3,2,1,0:T(4,128)S(1)}, f32[2,4,4,2048]{3,2,1,0:T(4,128)S(1)}, u32[]{:S(2)}, u32[]{:S(2)}) %collective-permute-start.3) | collective-permute-done | bytes 262176 | tf_op jit(solution)/shard_map/ppermute | solution.py:28
  205.7 4.9 %collective-permute-done.2 = f32[2,4,4,2048]{3,2,1,0:T(4,128)S(1)} collective-permute-done((f32[2,4,4,2048]{3,2,1,0:T(4,128)S(1)}, f32[2,4,4,2048]{3,2,1,0:T(4,128)S(1)}, u32[]{:S(2)}, u32[]{:S(2)}) %collective-permute-start.2) | collective-permute-done | bytes 262176 | tf_op jit(solution)/shard_map/ppermute | solution.py:26
  210.6 0.2 pad_maximum_fusion.5
  211.2 0.1 fusion.137
  211.6 0.1 fusion.141
  211.8 0.5 conditional.3
  211.8 0.2 fusion.24
  212.2 1.0 multiply_bitcast_fusion
  213.3 2.3 slice.842
  215.5 2.3 slice.843
  219.0 2.7 copy.7
  221.7 56.9 %gather_fusion.4 = f32[16384,4]{1,0:T(8,128)} fusion(f32[4,8192]{0,1:T(8,128)} %bitcast.129, s32[16384]{0:T(1024)S(1)} %broadcast_clamp_fusion), kind=kCustom, calls=%fused_computation.4 | custom fusion | bytes 589824 | tf_op jit(solution)/shard_map/jit(_take)/gather | solution.py:141
  278.6 5.2 %copy.8 = f32[4,8,2048]{2,0,1:T(4,128)S(1)} copy(f32[4,8,2048]{0,2,1:T(8,128)} %bitcast.130) | data formatting | bytes 524288 | tf_op jit(solution)/shard_map/jit(_take)/gather | solution.py:141
  283.9 0.1 select_select_fusion
  284.0 13.9 %all_to_all.16 = f32[4,8,2048]{2,0,1:T(4,128)S(1)} all-to-all(f32[4,8,2048]{2,0,1:T(4,128)S(1)} %select_select_fusion), channel_id=1, replica_groups=mesh['grp'=4,'tile'=8] {'tile'}, dimensions={1} | all-to-all | bytes 524288 | tf_op jit(solution)/shard_map/all_to_all | solution.py:143
  298.4 0.7 pad_maximum_fusion.8
  299.2 14.9 %all-gather.3.cloned.1.call-done = f32[128,2048]{1,0:T(8,128)} async-done(((f32[32,2048]{1,0:T(8,128)}), f32[128,2048]{1,0:T(8,128)}) %all-gather.3.cloned.1.call-update) | async-done | bytes 1048592 | tf_op jit(solution)/shard_map/all_gather | solution.py:145
  314.1 1.9 fusion.48
  (166 shorter events, 3.8 us)
Async XLA Ops:
  6.5 22.1 %copy-start = (s32[8192,1]{0,1:T(1,128)S(1)}, s32[8192,1]{0,1:T(1,128)}, u32[]{:S(2)}) copy-start(s32[8192,1]{0,1:T(1,128)} %param.15) | copy-start | bytes 98308
  6.5 307.6 %all-gather.3.cloned.1.call-start = ((), (), s32[]{:S(2)}) async-start(), calls=%async_computation.1 | async-start | bytes 1310720 | tf_op jit(solution)/shard_map/all_gather | solution.py:145
  16.5 168.0 %collective-permute-start.1 = (f32[2,4,4,2048]{3,2,1,0:T(4,128)S(1)}, f32[2,4,4,2048]{3,2,1,0:T(4,128)S(1)}, u32[]{:S(2)}, u32[]{:S(2)}) collective-permute-start(f32[2,4,4,2048]{3,2,1,0:T(4,128)S(1)} %pad_maximum_fusion.6), channel_id=1, source_target_pairs={{1,0},{2,1},{3,2},{4,3},{5,4},{6,5},{7,6},{0,7},{9,8},{10,9},{11,1... | collective-permute-start | bytes 786440 | tf_op jit(solution)/shard_map/ppermute | solution.py:28
  21.1 163.4 %collective-permute-start = (f32[2,4,4,2048]{3,2,1,0:T(4,128)S(1)}, f32[2,4,4,2048]{3,2,1,0:T(4,128)S(1)}, u32[]{:S(2)}, u32[]{:S(2)}) collective-permute-start(f32[2,4,4,2048]{3,2,1,0:T(4,128)S(1)} %pad_maximum_fusion.6), channel_id=1, source_target_pairs={{0,1},{1,2},{2,3},{3,4},{4,5},{5,6},{6,7},{7,0},{8,9},{9,10},{10,1... | collective-permute-start | bytes 786440 | tf_op jit(solution)/shard_map/ppermute | solution.py:26
  93.8 90.7 %copy-start.1 = (f32[1,4,4,2048]{3,2,1,0:T(4,128)S(1)}, f32[1,4,4,2048]{3,2,1,0:T(4,128)}, u32[]{:S(2)}) copy-start(f32[1,4,4,2048]{3,2,1,0:T(4,128)} %param.14) | copy-start | bytes 393220
  194.9 10.8 %collective-permute-start.3 = (f32[2,4,4,2048]{3,2,1,0:T(4,128)S(1)}, f32[2,4,4,2048]{3,2,1,0:T(4,128)S(1)}, u32[]{:S(2)}, u32[]{:S(2)}) collective-permute-start(f32[2,4,4,2048]{3,2,1,0:T(4,128)S(1)} %pad_maximum_fusion.7), channel_id=1, source_target_pairs={{1,0},{2,1},{3,2},{4,3},{5,4},{6,5},{7,6},{0,7},{9,8},{10,9},{11,1... | collective-permute-start | bytes 786440 | tf_op jit(solution)/shard_map/ppermute | solution.py:28
  199.6 11.0 %collective-permute-start.2 = (f32[2,4,4,2048]{3,2,1,0:T(4,128)S(1)}, f32[2,4,4,2048]{3,2,1,0:T(4,128)S(1)}, u32[]{:S(2)}, u32[]{:S(2)}) collective-permute-start(f32[2,4,4,2048]{3,2,1,0:T(4,128)S(1)} %pad_maximum_fusion.7), channel_id=1, source_target_pairs={{0,1},{1,2},{2,3},{3,4},{4,5},{5,6},{6,7},{7,0},{8,9},{9,10},{10,1... | collective-permute-start | bytes 786440 | tf_op jit(solution)/shard_map/ppermute | solution.py:26
Sparse Core Ops, SparseCore 0:
  299.3 14.7 all-gather.2
where the time goes:
time: 323 us
  local copies, waits for them, and re-layouts  226 us (70%)
  blocking collectives  30.7 us (10%)
  waiting for transfers between devices  25.8 us (8%)
  other arithmetic  16 us (5%)
  between operations  14 us (4%)
  starting transfers between devices  9.35 us (3%)
    gather x2, local copies, waits for them, and re-layouts, line_slots(): chosen = sorted_lines[position]  90.6 us
    gather x2, local copies, waits for them, and re-layouts, body(): outgoing = jnp.take(line_table, chosen.reshape(-1), axis=1)  62.2 us
    gather x1, local copies, waits for them, and re-layouts, line_slots(): sorted_owner = owners[sorted_lines]  45.5 us
    all_gather x2, blocking collectives, section_tendency(): fields = lax.all_gather(current, 'grp', axis=0, tiled=True)  16.8 us
    all_gather x1, waiting for transfers between devices, body(): all_coeffs = lax.all_gather(record[None], 'grp', axis=0, tiled=True)  14.9 us
    all_to_all x1, blocking collectives, body(): lax.all_to_all(outgoing, 'tile', split_axis=1, concat_axis=0, tiled=True)  13.9 us
    ppermute x2, starting transfers between devices, with_halo(): lax.ppermute(head, axis, [((i + 1) % count, i) for i in range(count)])  9.34 us
    gather x14, local copies, waits for them, and re-layouts, line_slots(): ends_at = jnp.searchsorted(sorted_owner, targets, side='right')  8.9 us
  transfers between devices with their start and end apart: 5, of which 3 were waited for; matrix products, arithmetic and copies ran while one was open for 50% of the time, Pallas kernels for 0%

commit v1 on v0

v1 whole, which is shorter than its diff:
```python
import functools

import jax
import jax.numpy as jnp
import numpy as np
from jax import lax
from jax.experimental import pallas as pl
from jax.experimental.pallas import tpu as pltpu
from jax.sharding import PartitionSpec as P

time_step = 0.2
viscosity = 0.05
reach = 4
first_coeffs = (0.8, -0.2, 4.0 / 105.0, -1.0 / 280.0)
second_center = -205.0 / 72.0
second_coeffs = (1.6, -0.2, 8.0 / 315.0, -1.0 / 560.0)
lift_alpha = -1.586134342059924
lift_beta = -0.052980118572961
lift_gamma = 0.882911075530934
lift_delta = 0.443506852043971
lift_scale = 1.149604398860241
LANES = 128
MESH = pl.DeviceIdType.MESH


def lift_numpy(signal):
    even, odd = signal[0::2].copy(), signal[1::2].copy()
    odd += lift_alpha * (even + np.roll(even, -1, 0))
    even += lift_beta * (odd + np.roll(odd, 1, 0))
    odd += lift_gamma * (even + np.roll(even, -1, 0))
    even += lift_delta * (odd + np.roll(odd, 1, 0))
    return np.concatenate([even * lift_scale, odd / lift_scale])


def lift_matrix(length):
    return lift_numpy(np.eye(length))


def band_matrix():
    full = lift_matrix(8 * LANES)
    low = full[LANES : 2 * LANES, LANES : 5 * LANES]
    high = full[4 * LANES + LANES : 4 * LANES + 2 * LANES, LANES : 5 * LANES]
    return np.concatenate([low, high]).T.astype(np.float32)


def shifted_y(value, k):
    return pltpu.roll(value, (-k) % value.shape[-1], value.ndim - 1)


def derivatives(center, shift, want_first=True, want_second=True):
    first, second = None, second_center * center if want_second else None
    for k in range(1, reach + 1):
        ahead, behind = shift(k), shift(-k)
        if want_first:
            term = first_coeffs[k - 1] * (ahead - behind)
            first = term if first is None else first + term
        if want_second:
            second = second + second_coeffs[k - 1] * (ahead + behind)
    return first, second


def flow_kernel(n_tile, own_ref, band_ref, out_ref, fields, mids, halo, mid_halo, pad, ppad, middle, fin,
                send_sem, recv_sem, hsend_sem, hrecv_sem, msend_sem, mrecv_sem, mhsend_sem, mhrecv_sem):
    g, t = lax.axis_index("grp"), lax.axis_index("tile")
    right, left = lax.rem(t + 1, n_tile), lax.rem(t + n_tile - 1, n_tile)
    planes, rows, ny = own_ref.shape[1:]
    own = own_ref.at[0]

    def gather_copy(src, dst, ssem, rsem, k, slot):
        return pltpu.make_async_remote_copy(
            src_ref=src, dst_ref=dst.at[slot], send_sem=ssem.at[k], recv_sem=rsem.at[slot],
            device_id=(k, t), device_id_type=MESH)

    def halo_copy(src, dst, ssem, rsem, side, slot, group):
        return pltpu.make_async_remote_copy(
            src_ref=src, dst_ref=dst.at[slot + side], send_sem=ssem.at[side], recv_sem=rsem.at[slot + side],
            device_id=(group, right if side == 0 else left), device_id_type=MESH)

    @pl.when(g < 3)
    def _():
        for side in range(2):
            halo_copy(own, halo, hsend_sem, hrecv_sem, side, 0, g).start()

    for k in range(3):
        @pl.when(g != k)
        def _(k=k):
            gather_copy(own, fields, send_sem, recv_sem, k, g).start()

    @pl.when(g == 3)
    def _():
        for side in range(2):
            halo_copy(own, halo, hsend_sem, hrecv_sem, side, 2, 0).start()

    @pl.when(g < 3)
    def _():
        for k in range(3):
            @pl.when(g == k)
            def _(k=k):
                fields[k] = own_ref[0]

        for z in range(planes):
            pad[z, reach : reach + rows] = own_ref[0, z]

        for k in range(4):
            @pl.when(g != k)
            def _(k=k):
                gather_copy(own, fields, send_sem, recv_sem, 0, k).wait_recv()
        for side in range(2):
            halo_copy(own, halo, hsend_sem, hrecv_sem, side, 0, g).wait_recv()

        @pl.when(g == 0)
        def _():
            for side in range(2):
                halo_copy(own, halo, hsend_sem, hrecv_sem, side, 2, 0).wait_recv()
            for z in range(planes):
                ppad[z, 0:reach] = halo[2, z, rows - reach : rows]
                ppad[z, reach : reach + rows] = fields[3, z]
                ppad[z, reach + rows : 2 * reach + rows] = halo[3, z, 0:reach]
            for z in range(planes):
                middle[z], _ = derivatives(None, lambda k: ppad[z, reach + k : reach + k + rows], True, False)

        @pl.when(g == 1)
        def _():
            for z in range(planes):
                value = fields[3, z]
                middle[z], _ = derivatives(None, lambda k: shifted_y(value, k), True, False)

        @pl.when(g == 2)
        def _():
            for z in range(planes):
                middle[z], _ = derivatives(None, lambda k: fields[3, (z + k) % planes], True, False)

        def tendency(z, vel, press):
            center = pad[z, reach : reach + rows]
            fx, sx = derivatives(center, lambda k: pad[z, reach + k : reach + k + rows])
            fy, sy = derivatives(center, lambda k: shifted_y(center, k))
            fz, sz = derivatives(center, lambda k: pad[(z + k) % planes, reach : reach + rows])
            advect = vel[0, z] * fx + vel[1, z] * fy + vel[2, z] * fz
            return viscosity * (sx + sy + sz) - advect - press

        for z in range(planes):
            pad[z, 0:reach] = halo[0, z, rows - reach : rows]
            pad[z, reach + rows : 2 * reach + rows] = halo[1, z, 0:reach]
        for z in range(planes):
            press = middle[z]
            ppad[z, 0:rows] = press
        for z in range(planes):
            middle[z] = own_ref[0, z] + time_step * tendency(z, fields, ppad[z, 0:rows])

        for side in range(2):
            halo_copy(middle, mid_halo, mhsend_sem, mhrecv_sem, side, 0, g).start()
        for k in range(3):
            @pl.when(g != k)
            def _(k=k):
                gather_copy(middle, mids, msend_sem, mrecv_sem, k, g).start()

            @pl.when(g == k)
            def _(k=k):
                mids[k] = middle[...]

        for z in range(planes):
            pad[z, reach : reach + rows] = middle[z]
        for k in range(3):
            @pl.when(g != k)
            def _(k=k):
                gather_copy(middle, mids, msend_sem, mrecv_sem, 0, k).wait_recv()
        for side in range(2):
            halo_copy(middle, mid_halo, mhsend_sem, mhrecv_sem, side, 0, g).wait_recv()
        for z in range(planes):
            pad[z, 0:reach] = mid_halo[0, z, rows - reach : rows]
            pad[z, reach + rows : 2 * reach + rows] = mid_halo[1, z, 0:reach]
        for z in range(planes):
            fin[z] = 0.5 * ((own_ref[0, z] + middle[z]) + time_step * tendency(z, mids, ppad[z, 0:rows]))

        blocks = ny // (2 * LANES)
        groups = ny // LANES
        for z in range(planes):
            value = fin[z]
            pieces = []
            for b in range(blocks):
                window = [value[:, ((2 * b + j) % groups) * LANES : ((2 * b + j) % groups + 1) * LANES] for j in (-1, 0, 1, 2)]
                pieces.append(jnp.concatenate(window, axis=1))
            stacked = jnp.concatenate(pieces, axis=0)
            lifted = jnp.dot(stacked, band_ref[...], precision=lax.Precision.HIGHEST, preferred_element_type=jnp.float32)
            for b in range(blocks):
                piece = lifted[b * rows : (b + 1) * rows]
                fin[z, :, b * LANES : (b + 1) * LANES] = piece[:, 0:LANES]
                fin[z, :, ny // 2 + b * LANES : ny // 2 + (b + 1) * LANES] = piece[:, LANES:]

        half = planes // 2
        even = [fin[2 * i] for i in range(half)]
        odd = [fin[2 * i + 1] for i in range(half)]
        odd = [odd[i] + lift_alpha * (even[i] + even[(i + 1) % half]) for i in range(half)]
        even = [even[i] + lift_beta * (odd[i] + odd[(i - 1) % half]) for i in range(half)]
        odd = [odd[i] + lift_gamma * (even[i] + even[(i + 1) % half]) for i in range(half)]
        even = [even[i] + lift_delta * (odd[i] + odd[(i - 1) % half]) for i in range(half)]
        for i in range(half):
            out_ref[i] = even[i] * lift_scale
            out_ref[half + i] = odd[i] * (1.0 / lift_scale)

        for side in range(2):
            halo_copy(middle, mid_halo, mhsend_sem, mhrecv_sem, side, 0, g).wait_send()
        for k in range(3):
            @pl.when(g != k)
            def _(k=k):
                gather_copy(middle, mids, msend_sem, mrecv_sem, k, g).wait_send()

    @pl.when(g == 3)
    def _():
        out_ref[...] = jnp.zeros_like(out_ref)

    for side in range(2):
        halo_copy(own, halo, hsend_sem, hrecv_sem, side, 0, g).wait_send()
    for k in range(3):
        @pl.when(g != k)
        def _(k=k):
            gather_copy(own, fields, send_sem, recv_sem, k, g).wait_send()


def slots_kernel(n_tile, owner_ref, place_ref, base_ref, count_ref):
    owner = owner_ref[...]
    n_blocks = owner.shape[0]
    upper = (lax.broadcasted_iota(jnp.int32, (LANES, LANES), 0) <= lax.broadcasted_iota(jnp.int32, (LANES, LANES), 1)).astype(jnp.float32)
    lower = (lax.broadcasted_iota(jnp.int32, (n_blocks, n_blocks), 0) > lax.broadcasted_iota(jnp.int32, (n_blocks, n_blocks), 1)).astype(jnp.float32)
    lane = lax.broadcasted_iota(jnp.int32, (n_blocks, LANES), 1)

    def step(s, carry):
        place, counts, ahead = carry
        mask = (owner == s).astype(jnp.float32)
        within = jnp.dot(mask, upper, preferred_element_type=jnp.float32)
        total = jnp.sum(mask, axis=1, keepdims=True)
        place = place + mask * (ahead + within - 1.0)
        counts = jnp.where(lane == s, total, counts)
        return place, counts, ahead + total

    zeros = jnp.zeros((n_blocks, LANES), jnp.float32)
    carry = (zeros, zeros, jnp.zeros((n_blocks, 1), jnp.float32))
    if n_tile <= 16:
        for s in range(n_tile):
            carry = step(s, carry)
    else:
        carry = lax.fori_loop(0, n_tile, step, carry)
    place, counts, _ = carry
    place_ref[...] = place
    count_ref[...] = counts.astype(jnp.int32)
    base_ref[...] = jnp.dot(lower, counts, preferred_element_type=jnp.float32).astype(jnp.int32)


def compact_kernel(n_tile, base_ref, count_ref, coeff_ref, place_ref, out_ref, current):
    planes, rows, ny = coeff_ref.shape
    groups = ny // LANES
    out_ref[...] = jnp.zeros_like(out_ref)
    current[...] = jnp.zeros_like(current)
    rank = lax.broadcasted_iota(jnp.int32, (LANES, LANES), 0).astype(jnp.float32)
    lane = lax.broadcasted_iota(jnp.int32, (rows, LANES), 1)

    def block(b, _):
        z, y = b // groups, b % groups
        value = coeff_ref[z, :, pl.ds(pl.multiple_of(y * LANES, LANES), LANES)]
        high = value.astype(jnp.bfloat16).astype(jnp.float32)
        rest = value - high
        mid = rest.astype(jnp.bfloat16).astype(jnp.float32)
        low = rest - mid
        parts = jnp.concatenate([high, mid, low], axis=0).astype(jnp.bfloat16)
        chosen = jnp.where(rank == place_ref[pl.ds(b, 1), :], 1.0, 0.0).astype(jnp.bfloat16)
        ordered = lax.dot_general(parts, chosen, (((1,), (1,)), ((), ())), preferred_element_type=jnp.float32)
        ordered = (ordered[0:rows] + ordered[rows : 2 * rows]) + ordered[2 * rows : 3 * rows]

        def pencil(s, ahead):
            base, count = base_ref[b, s], count_ref[b, s]
            start = base & (LANES - 1)
            end = start + count
            turned = pltpu.roll(ordered, (start - ahead) & (LANES - 1), 1)
            now = current[s] + jnp.where((lane >= start) & (lane < end), turned, 0.0)
            group = pl.multiple_of(base - start, LANES)
            out_ref[s, :, pl.ds(group, LANES)] = now
            after = jnp.where(lane < end - LANES, turned, 0.0)
            keep = jnp.where(end >= LANES, after, now)
            current[s] = keep
            out_ref[s, :, pl.ds(group + LANES, LANES)] = after
            return ahead + count

        if n_tile <= 16:
            ahead = jnp.int32(0)
            for s in range(n_tile):
                ahead = pencil(s, ahead)
        else:
            lax.fori_loop(0, n_tile, pencil, jnp.int32(0))
        return 0

    lax.fori_loop(0, planes * groups, block, 0)


def record_kernel(n_tile, chunks, sent_ref, matrix_ref, out_ref, got, records, send_sem, recv_sem, rsend_sem, rrecv_sem):
    g, t = lax.axis_index("grp"), lax.axis_index("tile")
    rows, nx, cap = sent_ref.shape[1], out_ref.shape[0], out_ref.shape[1]
    width = cap // chunks

    def exchange(s, slot):
        return pltpu.make_async_remote_copy(
            src_ref=sent_ref.at[s, :, pl.ds(0, cap)], dst_ref=got.at[slot], send_sem=send_sem.at[s],
            recv_sem=recv_sem.at[slot], device_id=(g, s), device_id_type=MESH)

    def report(c, slot):
        part = pl.ds(c * width, width)
        return pltpu.make_async_remote_copy(
            src_ref=out_ref.at[:, part], dst_ref=records.at[slot, :, part], send_sem=rsend_sem.at[c],
            recv_sem=rrecv_sem.at[slot, c], device_id=(3, t), device_id_type=MESH)

    @pl.when(g < 3)
    def _():
        for k in range(1, n_tile):
            exchange(lax.rem(t + k, n_tile), t).start()
        got[t] = sent_ref[t, :, 0:cap]
        for k in range(1, n_tile):
            exchange(lax.rem(t + k, n_tile), lax.rem(t + k, n_tile)).wait_recv()
        matrix = matrix_ref[...]
        for c in range(chunks):
            value = got[:, :, c * width : (c + 1) * width].reshape(nx, width)
            out_ref[:, c * width : (c + 1) * width] = jnp.dot(
                matrix, value, precision=lax.Precision.HIGHEST, preferred_element_type=jnp.float32)
            report(c, g).start()
        for k in range(1, n_tile):
            exchange(lax.rem(t + k, n_tile), t).wait_send()
        for c in range(chunks):
            report(c, g).wait_send()

    @pl.when(g == 3)
    def _():
        for c in range(chunks):
            for k in range(3):
                report(c, k).wait_recv()
            part = slice(c * width, (c + 1) * width)
            first, second, third = records[0, :, part], records[1, :, part], records[2, :, part]
            out_ref[:, part] = first * first + second * second + third * third


def body(flow_state, line_owner, *, n_tile):
    _, planes, rows, ny = flow_state.shape
    n_lines = line_owner.shape[0]
    n_blocks = n_lines // LANES
    nx = rows * n_tile
    cap = 2 * planes * ny // n_tile
    vmem = pl.BlockSpec(memory_space=pltpu.VMEM)
    smem = pl.BlockSpec(memory_space=pltpu.SMEM)
    f32 = jnp.float32
    shape = jax.ShapeDtypeStruct
    limit = 56 * 1024 * 1024
    dma = pltpu.SemaphoreType.DMA
    owner = line_owner.reshape(n_blocks, LANES)
    place, base, count = pl.pallas_call(
        functools.partial(slots_kernel, n_tile),
        out_shape=(shape((n_blocks, LANES), f32), shape((n_blocks, LANES), jnp.int32), shape((n_blocks, LANES), jnp.int32)),
        in_specs=[vmem], out_specs=(vmem, vmem, vmem), name="slots",
    )(owner)
    tile = (planes, rows, ny)
    coeffs = pl.pallas_call(
        functools.partial(flow_kernel, n_tile),
        out_shape=shape(tile, f32),
        in_specs=[vmem, vmem], out_specs=vmem,
        scratch_shapes=[
            pltpu.VMEM((4,) + tile, f32), pltpu.VMEM((3,) + tile, f32),
            pltpu.VMEM((4,) + tile, f32), pltpu.VMEM((2,) + tile, f32),
            pltpu.VMEM((planes, rows + 2 * reach, ny), f32), pltpu.VMEM((planes, rows + 2 * reach, ny), f32),
            pltpu.VMEM(tile, f32), pltpu.VMEM(tile, f32),
            dma((4,)), dma((4,)), dma((2,)), dma((4,)), dma((4,)), dma((4,)), dma((2,)), dma((2,)),
        ],
        compiler_params=pltpu.CompilerParams(has_side_effects=True, vmem_limit_bytes=limit), name="flow",
    )(flow_state, jnp.asarray(band_matrix()))
    sent = pl.pallas_call(
        functools.partial(compact_kernel, n_tile),
        out_shape=shape((n_tile, rows, cap + 2 * LANES), f32),
        in_specs=[smem, smem, vmem, vmem], out_specs=vmem,
        scratch_shapes=[pltpu.VMEM((n_tile, rows, LANES), f32)],
        compiler_params=pltpu.CompilerParams(vmem_limit_bytes=limit), name="compact",
    )(base, count, coeffs, place)
    chunks = 4 if cap % (4 * LANES) == 0 else 1
    record = pl.pallas_call(
        functools.partial(record_kernel, n_tile, chunks),
        out_shape=shape((nx, cap), f32),
        in_specs=[vmem, vmem], out_specs=vmem,
        scratch_shapes=[
            pltpu.VMEM((n_tile, rows, cap), f32), pltpu.VMEM((3, nx, cap), f32),
            dma((n_tile,)), dma((n_tile,)), dma((chunks,)), dma((3, chunks)),
        ],
        compiler_params=pltpu.CompilerParams(has_side_effects=True, vmem_limit_bytes=limit), name="record",
    )(sent, jnp.asarray(lift_matrix(nx).astype(np.float32)))
    return record[None, None]


def solution(mesh):
    in_specs = (P("grp", None, "tile", None), P())
    out_specs = P("grp", "tile", None, None)
    run = functools.partial(body, n_tile=mesh.shape["tile"])
    return jax.shard_map(run, mesh=mesh, in_specs=in_specs, out_specs=out_specs, check_vma=False)
```

time: 323 us -> 71.7 us (0.22)
  local copies, waits for them, and re-layouts: 226 us -> 1.67 us
  Pallas kernels: 0 us -> 68.7 us
  blocking collectives: 30.7 us -> 0 us
  waiting for transfers between devices: 25.8 us -> 0 us
  other arithmetic: 16 us -> 0 us
  between operations: 14 us -> 0.02 us
  starting transfers between devices: 9.35 us -> 0 us
    gather x33 -> x0, local copies, waits for them, and re-layouts: 216 us -> none  [the longest x2 90.6 us: line_slots(): chosen = sorted_lines[position]]
    pallas_call x0 -> x4, Pallas kernels: none -> 68.7 us  [the longest x1 32.1 us: body(): pl.pallas_call(functools.partial(flow_kernel, n_tile), out_shape=shape(ti...]
    all_gather x2 -> x0, blocking collectives: 16.8 us -> none  [section_tendency(): fields = lax.all_gather(current, 'grp', axis=0, tiled=True)]
    all_gather x1 -> x0, waiting for transfers between devices: 14.9 us -> none  [body(): all_coeffs = lax.all_gather(record[None], 'grp', axis=0, tiled=True)]
    all_to_all x1 -> x0, blocking collectives: 13.9 us -> none  [body(): lax.all_to_all(outgoing, 'tile', split_axis=1, concat_axis=0, tiled=True)]
    ppermute x4 -> x0, waiting for transfers between devices: 10.9 us -> none  [the longest x2 5.99 us: with_halo(): lax.ppermute(head, axis, [((i + 1) % count, i) for i in range(count)])]
    ppermute x4 -> x0, starting transfers between devices: 9.35 us -> none  [the longest x2 9.34 us: with_halo(): lax.ppermute(head, axis, [((i + 1) % count, i) for i in range(count)])]
    sort x1 -> x0, other arithmetic: 7.52 us -> none  [line_slots(): sorted_lines = jnp.argsort(owners, stable=True)]
  transfers between devices with their start and end apart: 5 -> 0, of which waited for: 3 -> 0; matrix products, arithmetic and copies ran while one was open for 50% -> 0% of each run, Pallas kernels for 0% -> 0%
where the time goes in v1:
time: 71.7 us; the launch traced here: 70.4 us
  Pallas kernels  68.7 us (96%)
  local copies, waits for them, and re-layouts  1.67 us (2%)
    pallas_call x1, Pallas kernels, body(): pl.pallas_call(functools.partial(flow_kernel, n_tile), out_shape=shape(ti...  32.1 us
    pallas_call x1, Pallas kernels, body(): pl.pallas_call(functools.partial(record_kernel, n_tile, chunks), out_shap...  17.7 us
    pallas_call x1, Pallas kernels, body(): pl.pallas_call(functools.partial(compact_kernel, n_tile), out_shape=shape...  17.3 us
    unnamed x1, local copies, waits for them, and re-layouts  1.67 us
    pallas_call x1, Pallas kernels, body(): pl.pallas_call(functools.partial(slots_kernel, n_tile), out_shape=(shape(...  1.65 us

profile of v1, /device:TPU:0, one launch (start us, length us, event | category | flops | bytes accessed | tf_op | source)
XLA Modules:
  0.0 70.4 jit_solution(13622317810842754120)
XLA Ops:
  0.0 1.7 %slots.1 = (f32[64,128]{1,0:T(8,128)}, s32[64,128]{1,0:T(8,128)}, s32[64,128]{1,0:T(8,128)}) custom-call(s32[64,128]{1,0:T(8,128)} %bitcast.3), custom_call_target="tpu_custom_call" | custom-call | tf_op jit(solution)/shard_map/slots/pallas_call | solution.py:351
  1.7 32.1 %flow.1.coeff_ref = f32[4,4,2048]{2,1,0:T(4,128)} custom-call(f32[1,4,4,2048]{3,2,1,0:T(4,128)} %own_ref.1, f32[512,256]{1,0:T(8,128)} %constant.4.clone.band_ref), custom_call_target="tpu_custom_call" | custom-call | tf_op jit(solution)/shard_map/flow/pallas_call | solution.py:357
  33.8 17.3 %compact.1.sent_ref = f32[8,4,2304]{2,1,0:T(4,128)} custom-call(s32[64,128]{1,0:T(8,128)} %get-tuple-element.8.base_ref, s32[64,128]{1,0:T(8,128)} %get-tuple-element.9.count_ref, f32[4,4,2048]{2,1,0:T(4,128)} %flow.1.coeff_ref, f32[64,128]{1,0:T(8,128)} %get-tuple-element.10.place_ref), custom_call_target="tpu_custom_call" | custom-call | tf_op jit(solution)/shard_map/compact/pallas_call | solution.py:370
  51.0 17.7 %record.1 = f32[32,2048]{1,0:T(8,128)} custom-call(f32[8,4,2304]{2,1,0:T(4,128)} %compact.1.sent_ref, f32[32,32]{1,0:T(8,128)} %constant.5.clone.matrix_ref), custom_call_target="tpu_custom_call" | custom-call | tf_op jit(solution)/shard_map/record/pallas_call | solution.py:378
  68.7 1.7 %copy.6 = f32[1,1,32,2048]{3,2,1,0:T(8,128)} copy(f32[1,1,32,2048]{3,2,1,0:T(8,128)} %bitcast.2) | data formatting | bytes 524288

commit v2 on v1

--- a/solution.py
+++ b/solution.py
@@ -59,13 +59,58 @@
     return first, second
 
 
-def flow_kernel(n_tile, own_ref, band_ref, out_ref, fields, mids, halo, mid_halo, pad, ppad, middle, fin,
-                send_sem, recv_sem, hsend_sem, hrecv_sem, msend_sem, mrecv_sem, mhsend_sem, mhrecv_sem):
+def slots_of(n_tile, owner_ref, place_ref, base_ref, count_ref):
+    owner = owner_ref[...]
+    n_blocks = owner.shape[0]
+    upper = (lax.broadcasted_iota(jnp.int32, (LANES, LANES), 0) <= lax.broadcasted_iota(jnp.int32, (LANES, LANES), 1)).astype(jnp.float32)
+    lower = (lax.broadcasted_iota(jnp.int32, (n_blocks, n_blocks), 0) > lax.broadcasted_iota(jnp.int32, (n_blocks, n_blocks), 1)).astype(jnp.float32)
+    lane = lax.broadcasted_iota(jnp.int32, (n_blocks, LANES), 1)
+
+    def step(s, carry):
+        place, counts, ahead = carry
+        mask = (owner == s).astype(jnp.float32)
+        within = jnp.dot(mask, upper, preferred_element_type=jnp.float32)
+        total = jnp.sum(mask, axis=1, keepdims=True)
+        place = place + mask * (ahead + within - 1.0)
+        counts = jnp.where(lane == s, total, counts)
+        return place, counts, ahead + total
+
+    zeros = jnp.zeros((n_blocks, LANES), jnp.float32)
+    carry = (zeros, zeros, jnp.zeros((n_blocks, 1), jnp.float32))
+    if n_tile <= 16:
+        for s in range(n_tile):
+            carry = step(s, carry)
+    else:
+        carry = lax.fori_loop(0, n_tile, step, carry)
+    place, counts, _ = carry
+    place_ref[...] = place
+    count_ref[...] = counts.astype(jnp.int32)
+    base_ref[...] = jnp.dot(lower, counts, preferred_element_type=jnp.float32).astype(jnp.int32)
+
+
+def flow_kernel(n_tile, own_ref, band_ref, owner_ref, out_ref, place_ref, base_ref, count_ref,
+                fields, mids, halo, mid_halo, pad, ppad, middle, fin, along_y, along_z, lap, send_sem, recv_sem, hsend_sem, hrecv_sem, msend_sem, mrecv_sem, mhsend_sem, mhrecv_sem):
     g, t = lax.axis_index("grp"), lax.axis_index("tile")
     right, left = lax.rem(t + 1, n_tile), lax.rem(t + n_tile - 1, n_tile)
     planes, rows, ny = own_ref.shape[1:]
     own = own_ref.at[0]
 
+    barrier = pltpu.get_barrier_semaphore()
+    for k in range(1, 4):
+        pl.semaphore_signal(barrier, inc=1, device_id=(lax.rem(g + k, 4), t), device_id_type=MESH)
+    for side in (right, left):
+        pl.semaphore_signal(barrier, inc=1, device_id=(g, side), device_id_type=MESH)
+
+    @pl.when((g == 0) | (g == 3))
+    def _():
+        for side in (right, left):
+            pl.semaphore_signal(barrier, inc=1, device_id=(3 - g, side), device_id_type=MESH)
+        pl.semaphore_wait(barrier, 7)
+
+    @pl.when((g == 1) | (g == 2))
+    def _():
+        pl.semaphore_wait(barrier, 5)
+
     def gather_copy(src, dst, ssem, rsem, k, slot):
         return pltpu.make_async_remote_copy(
             src_ref=src, dst_ref=dst.at[slot], send_sem=ssem.at[k], recv_sem=rsem.at[slot],
@@ -91,6 +136,15 @@
         for side in range(2):
             halo_copy(own, halo, hsend_sem, hrecv_sem, side, 2, 0).start()
 
+    def local_terms():
+        for z in range(planes):
+            center = pad[z, reach : reach + rows]
+            fy, sy = derivatives(center, lambda k: shifted_y(center, k))
+            fz, sz = derivatives(center, lambda k: pad[(z + k) % planes, reach : reach + rows])
+            along_y[z], along_z[z], lap[z] = fy, fz, sy + sz
+
+    slots_of(n_tile, owner_ref, place_ref, base_ref, count_ref)
+
     @pl.when(g < 3)
     def _():
         for k in range(3):
@@ -100,6 +154,7 @@
 
         for z in range(planes):
             pad[z, reach : reach + rows] = own_ref[0, z]
+        local_terms()
 
         for k in range(4):
             @pl.when(g != k)
@@ -133,10 +188,8 @@
         def tendency(z, vel, press):
             center = pad[z, reach : reach + rows]
             fx, sx = derivatives(center, lambda k: pad[z, reach + k : reach + k + rows])
-            fy, sy = derivatives(center, lambda k: shifted_y(center, k))
-            fz, sz = derivatives(center, lambda k: pad[(z + k) % planes, reach : reach + rows])
-            advect = vel[0, z] * fx + vel[1, z] * fy + vel[2, z] * fz
-            return viscosity * (sx + sy + sz) - advect - press
+            advect = vel[0, z] * fx + vel[1, z] * along_y[z] + vel[2, z] * along_z[z]
+            return viscosity * (sx + lap[z]) - advect - press
 
         for z in range(planes):
             pad[z, 0:reach] = halo[0, z, rows - reach : rows]
@@ -160,6 +213,7 @@
 
         for z in range(planes):
             pad[z, reach : reach + rows] = middle[z]
+        local_terms()
         for k in range(3):
             @pl.when(g != k)
             def _(k=k):
@@ -217,35 +271,6 @@
             gather_copy(own, fields, send_sem, recv_sem, k, g).wait_send()
 
 
-def slots_kernel(n_tile, owner_ref, place_ref, base_ref, count_ref):
-    owner = owner_ref[...]
-    n_blocks = owner.shape[0]
-    upper = (lax.broadcasted_iota(jnp.int32, (LANES, LANES), 0) <= lax.broadcasted_iota(jnp.int32, (LANES, LANES), 1)).astype(jnp.float32)
-    lower = (lax.broadcasted_iota(jnp.int32, (n_blocks, n_blocks), 0) > lax.broadcasted_iota(jnp.int32, (n_blocks, n_blocks), 1)).astype(jnp.float32)
-    lane = lax.broadcasted_iota(jnp.int32, (n_blocks, LANES), 1)
-
-    def step(s, carry):
-        place, counts, ahead = carry
-        mask = (owner == s).astype(jnp.float32)
-        within = jnp.dot(mask, upper, preferred_element_type=jnp.float32)
-        total = jnp.sum(mask, axis=1, keepdims=True)
-        place = place + mask * (ahead + within - 1.0)
-        counts = jnp.where(lane == s, total, counts)
-        return place, counts, ahead + total
-
-    zeros = jnp.zeros((n_blocks, LANES), jnp.float32)
-    carry = (zeros, zeros, jnp.zeros((n_blocks, 1), jnp.float32))
-    if n_tile <= 16:
-        for s in range(n_tile):
-            carry = step(s, carry)
-    else:
-        carry = lax.fori_loop(0, n_tile, step, carry)
-    place, counts, _ = carry
-    place_ref[...] = place
-    count_ref[...] = counts.astype(jnp.int32)
-    base_ref[...] = jnp.dot(lower, counts, preferred_element_type=jnp.float32).astype(jnp.int32)
-
-
 def compact_kernel(n_tile, base_ref, count_ref, coeff_ref, place_ref, out_ref, current):
     planes, rows, ny = coeff_ref.shape
     groups = ny // LANES
@@ -254,7 +279,7 @@
     rank = lax.broadcasted_iota(jnp.int32, (LANES, LANES), 0).astype(jnp.float32)
     lane = lax.broadcasted_iota(jnp.int32, (rows, LANES), 1)
 
-    def block(b, _):
+    def sort(b):
         z, y = b // groups, b % groups
         value = coeff_ref[z, :, pl.ds(pl.multiple_of(y * LANES, LANES), LANES)]
         high = value.astype(jnp.bfloat16).astype(jnp.float32)
@@ -264,31 +289,36 @@
         parts = jnp.concatenate([high, mid, low], axis=0).astype(jnp.bfloat16)
         chosen = jnp.where(rank == place_ref[pl.ds(b, 1), :], 1.0, 0.0).astype(jnp.bfloat16)
         ordered = lax.dot_general(parts, chosen, (((1,), (1,)), ((), ())), preferred_element_type=jnp.float32)
-        ordered = (ordered[0:rows] + ordered[rows : 2 * rows]) + ordered[2 * rows : 3 * rows]
-
-        def pencil(s, ahead):
-            base, count = base_ref[b, s], count_ref[b, s]
-            start = base & (LANES - 1)
-            end = start + count
-            turned = pltpu.roll(ordered, (start - ahead) & (LANES - 1), 1)
-            now = current[s] + jnp.where((lane >= start) & (lane < end), turned, 0.0)
-            group = pl.multiple_of(base - start, LANES)
-            out_ref[s, :, pl.ds(group, LANES)] = now
-            after = jnp.where(lane < end - LANES, turned, 0.0)
-            keep = jnp.where(end >= LANES, after, now)
-            current[s] = keep
-            out_ref[s, :, pl.ds(group + LANES, LANES)] = after
-            return ahead + count
-
-        if n_tile <= 16:
-            ahead = jnp.int32(0)
-            for s in range(n_tile):
-                ahead = pencil(s, ahead)
-        else:
-            lax.fori_loop(0, n_tile, pencil, jnp.int32(0))
+        return (ordered[0:rows] + ordered[rows : 2 * rows]) + ordered[2 * rows : 3 * rows]
+
+    def pencil(b, ordered, s, ahead):
+        base, count = base_ref[b, s], count_ref[b, s]
+        start = base & (LANES - 1)
+        end = start + count
+        turned = pltpu.roll(ordered, (start - ahead) & (LANES - 1), 1)
+        now = current[s] + jnp.where((lane >= start) & (lane < end), turned, 0.0)
+        group = pl.multiple_of(base - start, LANES)
+        after = jnp.where(lane < end - LANES, turned, 0.0)
+        current[s] = jnp.where(end >= LANES, after, now)
+        out_ref[s, :, pl.ds(group, 2 * LANES)] = jnp.concatenate([now, after], axis=1)
+        return ahead + count
+
+    n_blocks = planes * groups
+    batch = 8 if n_blocks % 8 == 0 and n_tile <= 16 else 1
+
+    def blocks(i, _):
+        ordered = [sort(i * batch + j) for j in range(batch)]
+        for j in range(batch):
+            b = i * batch + j
+            if n_tile <= 16:
+                ahead = jnp.int32(0)
+                for s in range(n_tile):
+                    ahead = pencil(b, ordered[j], s, ahead)
+            else:
+                lax.fori_loop(0, n_tile, lambda s, ahead: pencil(b, ordered[j], s, ahead), jnp.int32(0))
         return 0
 
-    lax.fori_loop(0, planes * groups, block, 0)
+    lax.fori_loop(0, n_blocks // batch, blocks, 0)
 
 
 def record_kernel(n_tile, chunks, sent_ref, matrix_ref, out_ref, got, records, send_sem, recv_sem, rsend_sem, rrecv_sem):
@@ -296,10 +326,26 @@
     rows, nx, cap = sent_ref.shape[1], out_ref.shape[0], out_ref.shape[1]
     width = cap // chunks
 
-    def exchange(s, slot):
+    barrier = pltpu.get_barrier_semaphore()
+
+    @pl.when(g < 3)
+    def _():
+        for k in range(1, n_tile):
+            pl.semaphore_signal(barrier, inc=1, device_id=(g, lax.rem(t + k, n_tile)), device_id_type=MESH)
+        pl.semaphore_signal(barrier, inc=1, device_id=(3, t), device_id_type=MESH)
+        pl.semaphore_wait(barrier, n_tile)
+
+    @pl.when(g == 3)
+    def _():
+        for k in range(3):
+            pl.semaphore_signal(barrier, inc=1, device_id=(k, t), device_id_type=MESH)
+        pl.semaphore_wait(barrier, 3)
+
+    def exchange(s, slot, c):
+        part = pl.ds(c * width, width)
         return pltpu.make_async_remote_copy(
-            src_ref=sent_ref.at[s, :, pl.ds(0, cap)], dst_ref=got.at[slot], send_sem=send_sem.at[s],
-            recv_sem=recv_sem.at[slot], device_id=(g, s), device_id_type=MESH)
+            src_ref=sent_ref.at[s, :, part], dst_ref=got.at[slot, :, part], send_sem=send_sem.at[s, c],
+            recv_sem=recv_sem.at[slot, c], device_id=(g, s), device_id_type=MESH)
 
     def report(c, slot):
         part = pl.ds(c * width, width)
@@ -309,20 +355,21 @@
 
     @pl.when(g < 3)
     def _():
-        for k in range(1, n_tile):
-            exchange(lax.rem(t + k, n_tile), t).start()
+        for c in range(chunks):
+            for k in range(1, n_tile):
+                exchange(lax.rem(t + k, n_tile), t, c).start()
         got[t] = sent_ref[t, :, 0:cap]
-        for k in range(1, n_tile):
-            exchange(lax.rem(t + k, n_tile), lax.rem(t + k, n_tile)).wait_recv()
         matrix = matrix_ref[...]
         for c in range(chunks):
+            for k in range(1, n_tile):
+                exchange(lax.rem(t + k, n_tile), lax.rem(t + k, n_tile), c).wait_recv()
             value = got[:, :, c * width : (c + 1) * width].reshape(nx, width)
             out_ref[:, c * width : (c + 1) * width] = jnp.dot(
                 matrix, value, precision=lax.Precision.HIGHEST, preferred_element_type=jnp.float32)
             report(c, g).start()
-        for k in range(1, n_tile):
-            exchange(lax.rem(t + k, n_tile), t).wait_send()
         for c in range(chunks):
+            for k in range(1, n_tile):
+                exchange(lax.rem(t + k, n_tile), t, c).wait_send()
             report(c, g).wait_send()
 
     @pl.when(g == 3)
@@ -348,25 +395,21 @@
     limit = 56 * 1024 * 1024
     dma = pltpu.SemaphoreType.DMA
     owner = line_owner.reshape(n_blocks, LANES)
-    place, base, count = pl.pallas_call(
-        functools.partial(slots_kernel, n_tile),
-        out_shape=(shape((n_blocks, LANES), f32), shape((n_blocks, LANES), jnp.int32), shape((n_blocks, LANES), jnp.int32)),
-        in_specs=[vmem], out_specs=(vmem, vmem, vmem), name="slots",
-    )(owner)
     tile = (planes, rows, ny)
-    coeffs = pl.pallas_call(
+    ints = shape((n_blocks, LANES), jnp.int32)
+    coeffs, place, base, count = pl.pallas_call(
         functools.partial(flow_kernel, n_tile),
-        out_shape=shape(tile, f32),
-        in_specs=[vmem, vmem], out_specs=vmem,
+        out_shape=(shape(tile, f32), shape((n_blocks, LANES), f32), ints, ints),
+        in_specs=[vmem, vmem, vmem], out_specs=(vmem, vmem, vmem, vmem),
         scratch_shapes=[
             pltpu.VMEM((4,) + tile, f32), pltpu.VMEM((3,) + tile, f32),
             pltpu.VMEM((4,) + tile, f32), pltpu.VMEM((2,) + tile, f32),
             pltpu.VMEM((planes, rows + 2 * reach, ny), f32), pltpu.VMEM((planes, rows + 2 * reach, ny), f32),
-            pltpu.VMEM(tile, f32), pltpu.VMEM(tile, f32),
+            pltpu.VMEM(tile, f32), pltpu.VMEM(tile, f32), pltpu.VMEM(tile, f32), pltpu.VMEM(tile, f32), pltpu.VMEM(tile, f32),
             dma((4,)), dma((4,)), dma((2,)), dma((4,)), dma((4,)), dma((4,)), dma((2,)), dma((2,)),
         ],
-        compiler_params=pltpu.CompilerParams(has_side_effects=True, vmem_limit_bytes=limit), name="flow",
-    )(flow_state, jnp.asarray(band_matrix()))
+        compiler_params=pltpu.CompilerParams(has_side_effects=True, collective_id=0, vmem_limit_bytes=limit), name="flow",
+    )(flow_state, jnp.asarray(band_matrix()), owner)
     sent = pl.pallas_call(
         functools.partial(compact_kernel, n_tile),
         out_shape=shape((n_tile, rows, cap + 2 * LANES), f32),
@@ -381,9 +424,9 @@
         in_specs=[vmem, vmem], out_specs=vmem,
         scratch_shapes=[
             pltpu.VMEM((n_tile, rows, cap), f32), pltpu.VMEM((3, nx, cap), f32),
-            dma((n_tile,)), dma((n_tile,)), dma((chunks,)), dma((3, chunks)),
+            dma((n_tile, chunks)), dma((n_tile, chunks)), dma((chunks,)), dma((3, chunks)),
         ],
-        compiler_params=pltpu.CompilerParams(has_side_effects=True, vmem_limit_bytes=limit), name="record",
+        compiler_params=pltpu.CompilerParams(has_side_effects=True, collective_id=1, vmem_limit_bytes=limit), name="record",
     )(sent, jnp.asarray(lift_matrix(nx).astype(np.float32)))
     return record[None, None]
 

time: 71.7 us -> 48.6 us (0.68); the launches traced: 70.4 us -> 48.3 us
  Pallas kernels: 68.7 us -> 46.6 us
    pallas_call x1, Pallas kernels: 17.3 us -> 6.24 us  [body(): pl.pallas_call(functools.partial(compact_kernel, n_tile), out_shape=shape...]
    pallas_call x2 -> x1, Pallas kernels: 33.7 us -> 27.2 us  [body(): pl.pallas_call(functools.partial(flow_kernel, n_tile), out_shape=(shape(t...]
    pallas_call x1, Pallas kernels: 17.7 us -> 13.2 us  [body(): pl.pallas_call(functools.partial(record_kernel, n_tile, chunks), out_shap...]
where the time goes in v2:
time: 48.6 us; the launch traced here: 48.3 us
  Pallas kernels  46.6 us (96%)
  local copies, waits for them, and re-layouts  1.67 us (3%)
    pallas_call x1, Pallas kernels, body(): pl.pallas_call(functools.partial(flow_kernel, n_tile), out_shape=(shape(t...  27.2 us
    pallas_call x1, Pallas kernels, body(): pl.pallas_call(functools.partial(record_kernel, n_tile, chunks), out_shap...  13.2 us
    pallas_call x1, Pallas kernels, body(): pl.pallas_call(functools.partial(compact_kernel, n_tile), out_shape=shape...  6.24 us
    unnamed x1, local copies, waits for them, and re-layouts  1.67 us

profile of v2, /device:TPU:0, one launch (start us, length us, event | category | flops | bytes accessed | tf_op | source)
XLA Modules:
  0.0 48.3 jit_solution(2534346266069781718)
XLA Ops:
  0.0 27.2 %flow.1 = (f32[4,4,2048]{2,1,0:T(4,128)}, f32[64,128]{1,0:T(8,128)}, s32[64,128]{1,0:T(8,128)}, s32[64,128]{1,0:T(8,128)}) custom-call(f32[1,4,4,2048]{3,2,1,0:T(4,128)} %own_ref.1, f32[512,256]{1,0:T(8,128)} %constant.4.clone.band_ref, s32[64,128]{1,0:T(8,128)} %bitcast.3), custom_call_target="tpu_custom_call" | custom-call | tf_op jit(solution)/shard_map/flow/pallas_call | solution.py:400
  27.2 6.2 %compact.1.sent_ref = f32[8,4,2304]{2,1,0:T(4,128)} custom-call(s32[64,128]{1,0:T(8,128)} %get-tuple-element.9.base_ref, s32[64,128]{1,0:T(8,128)} %get-tuple-element.10.count_ref, f32[4,4,2048]{2,1,0:T(4,128)} %get-tuple-element.11.coeff_ref, f32[64,128]{1,0:T(8,128)} %get-tuple-element.12.place_ref), custom_call_target="tpu_custom_call" | custom-call | tf_op jit(solution)/shard_map/compact/pallas_call | solution.py:413
  33.5 13.2 %record.1 = f32[32,2048]{1,0:T(8,128)} custom-call(f32[8,4,2304]{2,1,0:T(4,128)} %compact.1.sent_ref, f32[32,32]{1,0:T(8,128)} %constant.5.clone.matrix_ref), custom_call_target="tpu_custom_call" | custom-call | tf_op jit(solution)/shard_map/record/pallas_call | solution.py:421
  46.6 1.7 %copy.6 = f32[1,1,32,2048]{3,2,1,0:T(8,128)} copy(f32[1,1,32,2048]{3,2,1,0:T(8,128)} %bitcast.2) | data formatting | bytes 524288

commit v3 on v2

--- a/solution.py
+++ b/solution.py
@@ -89,7 +89,7 @@
 
 
 def flow_kernel(n_tile, own_ref, band_ref, owner_ref, out_ref, place_ref, base_ref, count_ref,
-                fields, mids, halo, mid_halo, pad, ppad, middle, fin, along_y, along_z, lap, send_sem, recv_sem, hsend_sem, hrecv_sem, msend_sem, mrecv_sem, mhsend_sem, mhrecv_sem):
+                fields, mids, halo, mid_halo, pad, ppad, middle, fin, along_y, along_z, lap, send_sem, recv_sem, hsend_sem, hrecv_sem, msend_sem, mrecv_sem, mhsend_sem, mhrecv_sem, relay_sem):
     g, t = lax.axis_index("grp"), lax.axis_index("tile")
     right, left = lax.rem(t + 1, n_tile), lax.rem(t + n_tile - 1, n_tile)
     planes, rows, ny = own_ref.shape[1:]
@@ -116,6 +116,25 @@
             src_ref=src, dst_ref=dst.at[slot], send_sem=ssem.at[k], recv_sem=rsem.at[slot],
             device_id=(k, t), device_id_type=MESH)
 
+    half = planes // 2
+
+    def whole_copy(k, slot):
+        return pltpu.make_async_remote_copy(
+            src_ref=own, dst_ref=fields.at[slot], send_sem=send_sem.at[k], recv_sem=recv_sem.at[slot, 0],
+            device_id=(k, t), device_id_type=MESH)
+
+    def half_copy(slot, k):
+        part = pl.ds(k * half, half)
+        return pltpu.make_async_remote_copy(
+            src_ref=own.at[part], dst_ref=fields.at[slot, part], send_sem=send_sem.at[k],
+            recv_sem=recv_sem.at[slot, k], device_id=(k, t), device_id_type=MESH)
+
+    def relay_copy(slot, k):
+        part = pl.ds(k * half, half)
+        return pltpu.make_async_remote_copy(
+            src_ref=fields.at[slot, part], dst_ref=fields.at[slot, part], send_sem=relay_sem.at[slot],
+            recv_sem=recv_sem.at[slot, k], device_id=(1 - k, t), device_id_type=MESH)
+
     def halo_copy(src, dst, ssem, rsem, side, slot, group):
         return pltpu.make_async_remote_copy(
             src_ref=src, dst_ref=dst.at[slot + side], send_sem=ssem.at[side], recv_sem=rsem.at[slot + side],
@@ -127,12 +146,18 @@
             halo_copy(own, halo, hsend_sem, hrecv_sem, side, 0, g).start()
 
     for k in range(3):
-        @pl.when(g != k)
+        @pl.when((g < 2) & (g != k))
         def _(k=k):
-            gather_copy(own, fields, send_sem, recv_sem, k, g).start()
+            whole_copy(k, g).start()
+
+    @pl.when(g >= 2)
+    def _():
+        for k in range(2):
+            half_copy(g, k).start()
 
     @pl.when(g == 3)
     def _():
+        whole_copy(2, 3).start()
         for side in range(2):
             halo_copy(own, halo, hsend_sem, hrecv_sem, side, 2, 0).start()
 
@@ -156,10 +181,20 @@
             pad[z, reach : reach + rows] = own_ref[0, z]
         local_terms()
 
-        for k in range(4):
-            @pl.when(g != k)
-            def _(k=k):
-                gather_copy(own, fields, send_sem, recv_sem, 0, k).wait_recv()
+        @pl.when(g < 2)
+        def _():
+            for slot in (2, 3):
+                half_copy(slot, g).wait_recv()
+                relay_copy(slot, g).start()
+            whole_copy(0, 1 - g).wait_recv()
+            for slot in (2, 3):
+                half_copy(slot, 1 - g).wait_recv()
+
+        @pl.when(g == 2)
+        def _():
+            for slot in (0, 1, 3):
+                whole_copy(0, slot).wait_recv()
+
         for side in range(2):
             halo_copy(own, halo, hsend_sem, hrecv_sem, side, 0, g).wait_recv()
 
@@ -241,7 +276,6 @@
                 fin[z, :, b * LANES : (b + 1) * LANES] = piece[:, 0:LANES]
                 fin[z, :, ny // 2 + b * LANES : ny // 2 + (b + 1) * LANES] = piece[:, LANES:]
 
-        half = planes // 2
         even = [fin[2 * i] for i in range(half)]
         odd = [fin[2 * i + 1] for i in range(half)]
         odd = [odd[i] + lift_alpha * (even[i] + even[(i + 1) % half]) for i in range(half)]
@@ -266,9 +300,23 @@
     for side in range(2):
         halo_copy(own, halo, hsend_sem, hrecv_sem, side, 0, g).wait_send()
     for k in range(3):
-        @pl.when(g != k)
+        @pl.when((g < 2) & (g != k))
         def _(k=k):
-            gather_copy(own, fields, send_sem, recv_sem, k, g).wait_send()
+            whole_copy(k, g).wait_send()
+
+    @pl.when(g < 2)
+    def _():
+        for slot in (2, 3):
+            relay_copy(slot, g).wait_send()
+
+    @pl.when(g >= 2)
+    def _():
+        for k in range(2):
+            half_copy(g, k).wait_send()
+
+    @pl.when(g == 3)
+    def _():
+        whole_copy(2, 3).wait_send()
 
 
 def compact_kernel(n_tile, base_ref, count_ref, coeff_ref, place_ref, out_ref, current):
@@ -392,7 +440,7 @@
     smem = pl.BlockSpec(memory_space=pltpu.SMEM)
     f32 = jnp.float32
     shape = jax.ShapeDtypeStruct
-    limit = 56 * 1024 * 1024
+    limit = 16 * 1024 * 1024
     dma = pltpu.SemaphoreType.DMA
     owner = line_owner.reshape(n_blocks, LANES)
     tile = (planes, rows, ny)
@@ -406,7 +454,7 @@
             pltpu.VMEM((4,) + tile, f32), pltpu.VMEM((2,) + tile, f32),
             pltpu.VMEM((planes, rows + 2 * reach, ny), f32), pltpu.VMEM((planes, rows + 2 * reach, ny), f32),
             pltpu.VMEM(tile, f32), pltpu.VMEM(tile, f32), pltpu.VMEM(tile, f32), pltpu.VMEM(tile, f32), pltpu.VMEM(tile, f32),
-            dma((4,)), dma((4,)), dma((2,)), dma((4,)), dma((4,)), dma((4,)), dma((2,)), dma((2,)),
+            dma((4,)), dma((4, 2)), dma((2,)), dma((4,)), dma((4,)), dma((4,)), dma((2,)), dma((2,)), dma((4,)),
         ],
         compiler_params=pltpu.CompilerParams(has_side_effects=True, collective_id=0, vmem_limit_bytes=limit), name="flow",
     )(flow_state, jnp.asarray(band_matrix()), owner)

time: 48.6 us -> 46.2 us (0.951)
  Pallas kernels: 46.6 us -> 42.5 us
  local copies, waits for them, and re-layouts: 1.67 us -> 3.41 us
    pallas_call x1, Pallas kernels: 27.2 us -> 23.9 us  [body(): pl.pallas_call(functools.partial(flow_kernel, n_tile), out_shape=(shape(t...]
    unnamed x1 -> x9, local copies, waits for them, and re-layouts: 1.67 us -> 3.41 us
    pallas_call x1, Pallas kernels: 6.24 us -> 5.47 us  [body(): pl.pallas_call(functools.partial(compact_kernel, n_tile), out_shape=shape...]
where the time goes in v3:
time: 46.2 us; the launch traced here: 45.9 us
  Pallas kernels  42.5 us (92%)
  local copies, waits for them, and re-layouts  3.41 us (7%)
    pallas_call x1, Pallas kernels, body(): pl.pallas_call(functools.partial(flow_kernel, n_tile), out_shape=(shape(t...  23.9 us
    pallas_call x1, Pallas kernels, body(): pl.pallas_call(functools.partial(record_kernel, n_tile, chunks), out_shap...  13.1 us
    pallas_call x1, Pallas kernels, body(): pl.pallas_call(functools.partial(compact_kernel, n_tile), out_shape=shape...  5.47 us
    unnamed x9, local copies, waits for them, and re-layouts  3.41 us

profile of v3, /device:TPU:0, one launch (start us, length us, event | category | flops | bytes accessed | tf_op | source)
XLA Modules:
  0.0 45.9 jit_solution(1613960255811951445)
XLA Ops:
  0.0 0.0 copy-start
  0.0 1.0 %copy-done = f32[512,256]{1,0:T(8,128)S(1)} copy-done((f32[512,256]{1,0:T(8,128)S(1)}, f32[512,256]{1,0:T(8,128)}, u32[]{:S(2)}) %copy-start) | copy-done | bytes 524312
  1.0 0.0 copy-start.1
  1.0 0.9 %copy-done.1 = f32[1,4,4,2048]{3,2,1,0:T(4,128)S(1)} copy-done((f32[1,4,4,2048]{3,2,1,0:T(4,128)S(1)}, f32[1,4,4,2048]{3,2,1,0:T(4,128)}, u32[]{:S(2)}) %copy-start.1) | copy-done | bytes 131096
  1.9 0.0 copy-start.2
  1.9 0.8 %copy-done.2 = s32[8192,1]{0,1:T(1,128)S(1)} copy-done((s32[8192,1]{0,1:T(1,128)S(1)}, s32[8192,1]{0,1:T(1,128)}, u32[]{:S(2)}) %copy-start.2) | copy-done | bytes 32792
  2.7 23.9 %flow.1 = (f32[4,4,2048]{2,1,0:T(4,128)S(1)}, f32[64,128]{1,0:T(8,128)S(1)}, s32[64,128]{1,0:T(8,128)S(1)}, s32[64,128]{1,0:T(8,128)S(1)}) custom-call(f32[1,4,4,2048]{3,2,1,0:T(4,128)S(1)} %copy-done.1, f32[512,256]{1,0:T(8,128)S(1)} %copy-done, s32[64,128]{1,0:T(8,128)S(1)} %bitcast.3), custom_call_target="tpu_custom_call" | custom-call | tf_op jit(solution)/shard_map/flow/pallas_call | solution.py:448
  26.6 0.0 copy-start.3
  26.6 5.5 %compact.1.sent_ref = f32[8,4,2304]{2,1,0:T(4,128)S(1)} custom-call(s32[64,128]{1,0:T(8,128)S(1)} %get-tuple-element.9.base_ref, s32[64,128]{1,0:T(8,128)S(1)} %get-tuple-element.10.count_ref, f32[4,4,2048]{2,1,0:T(4,128)S(1)} %get-tuple-element.11.coeff_ref, f32[64,128]{1,0:T(8,128)S(1)} %get-tuple-element.12.place_ref), custom_call_target="tpu_custom_call" | custom-call | tf_op jit(solution)/shard_map/compact/pallas_call | solution.py:461
  32.1 0.0 copy-done.3
  32.1 13.1 %record.1 = f32[32,2048]{1,0:T(8,128)S(1)} custom-call(f32[8,4,2304]{2,1,0:T(4,128)S(1)} %compact.1.sent_ref, f32[32,32]{1,0:T(8,128)S(1)} %copy-done.3), custom_call_target="tpu_custom_call" | custom-call | tf_op jit(solution)/shard_map/record/pallas_call | solution.py:469
  45.2 0.7 %copy.6 = f32[1,1,32,2048]{3,2,1,0:T(8,128)} copy(f32[1,1,32,2048]{3,2,1,0:T(8,128)S(1)} %bitcast.2) | data formatting | bytes 524288
Async XLA Ops:
  0.0 1.0 %copy-start = (f32[512,256]{1,0:T(8,128)S(1)}, f32[512,256]{1,0:T(8,128)}, u32[]{:S(2)}) copy-start(f32[512,256]{1,0:T(8,128)} %constant.4.clone.band_ref) | copy-start | bytes 1572868
  1.0 0.9 %copy-start.1 = (f32[1,4,4,2048]{3,2,1,0:T(4,128)S(1)}, f32[1,4,4,2048]{3,2,1,0:T(4,128)}, u32[]{:S(2)}) copy-start(f32[1,4,4,2048]{3,2,1,0:T(4,128)} %own_ref.1) | copy-start | bytes 393220
  1.9 0.8 %copy-start.2 = (s32[8192,1]{0,1:T(1,128)S(1)}, s32[8192,1]{0,1:T(1,128)}, u32[]{:S(2)}) copy-start(s32[8192,1]{0,1:T(1,128)} %param.5) | copy-start | bytes 98308
  26.6 5.5 %copy-start.3 = (f32[32,32]{1,0:T(8,128)S(1)}, f32[32,32]{1,0:T(8,128)}, u32[]{:S(2)}) copy-start(f32[32,32]{1,0:T(8,128)} %constant.5.clone.matrix_ref) | copy-start | bytes 12292

commit v4 on v3

--- a/solution.py
+++ b/solution.py
@@ -43,6 +43,24 @@
     return np.concatenate([low, high]).T.astype(np.float32)
 
 
+def band_value(taps_low, taps_high):
+    row = lax.broadcasted_iota(jnp.int32, (4 * LANES, 2 * LANES), 0)
+    column = lax.broadcasted_iota(jnp.int32, (4 * LANES, 2 * LANES), 1)
+    distance = row - LANES - 2 * (column & (LANES - 1))
+    is_low = column < LANES
+    value = jnp.zeros((4 * LANES, 2 * LANES), jnp.float32)
+    for offset in range(-4, 5):
+        tap = jnp.where(is_low, taps_low[offset + 4], taps_high[offset + 4])
+        value = jnp.where(distance == offset, tap, value)
+    return value
+
+
+def band_taps():
+    band = band_matrix()
+    rows = slice(LANES + LANES // 2 - 4, LANES + LANES // 2 + 5)
+    return [float(x) for x in band[rows, LANES // 4]], [float(x) for x in band[rows, LANES + LANES // 4]]
+
+
 def shifted_y(value, k):
     return pltpu.roll(value, (-k) % value.shape[-1], value.ndim - 1)
 
@@ -88,8 +106,8 @@
     base_ref[...] = jnp.dot(lower, counts, preferred_element_type=jnp.float32).astype(jnp.int32)
 
 
-def flow_kernel(n_tile, own_ref, band_ref, owner_ref, out_ref, place_ref, base_ref, count_ref,
-                fields, mids, halo, mid_halo, pad, ppad, middle, fin, along_y, along_z, lap, send_sem, recv_sem, hsend_sem, hrecv_sem, msend_sem, mrecv_sem, mhsend_sem, mhrecv_sem, relay_sem):
+def flow_kernel(n_tile, own_ref, owner_ref, out_ref, place_ref, base_ref, count_ref,
+                fields, mids, halo, mid_halo, pad, ppad, middle, fin, along_y, along_z, lap, send_sem, recv_sem, hsend_sem, hrecv_sem, msend_sem, mrecv_sem, mhsend_sem, mhrecv_sem, relay_sem, band_ref):
     g, t = lax.axis_index("grp"), lax.axis_index("tile")
     right, left = lax.rem(t + 1, n_tile), lax.rem(t + n_tile - 1, n_tile)
     planes, rows, ny = own_ref.shape[1:]
@@ -169,6 +187,7 @@
             along_y[z], along_z[z], lap[z] = fy, fz, sy + sz
 
     slots_of(n_tile, owner_ref, place_ref, base_ref, count_ref)
+    band_ref[...] = band_value(*band_taps())
 
     @pl.when(g < 3)
     def _():
@@ -448,16 +467,17 @@
     coeffs, place, base, count = pl.pallas_call(
         functools.partial(flow_kernel, n_tile),
         out_shape=(shape(tile, f32), shape((n_blocks, LANES), f32), ints, ints),
-        in_specs=[vmem, vmem, vmem], out_specs=(vmem, vmem, vmem, vmem),
+        in_specs=[vmem, vmem], out_specs=(vmem, vmem, vmem, vmem),
         scratch_shapes=[
             pltpu.VMEM((4,) + tile, f32), pltpu.VMEM((3,) + tile, f32),
             pltpu.VMEM((4,) + tile, f32), pltpu.VMEM((2,) + tile, f32),
             pltpu.VMEM((planes, rows + 2 * reach, ny), f32), pltpu.VMEM((planes, rows + 2 * reach, ny), f32),
             pltpu.VMEM(tile, f32), pltpu.VMEM(tile, f32), pltpu.VMEM(tile, f32), pltpu.VMEM(tile, f32), pltpu.VMEM(tile, f32),
             dma((4,)), dma((4, 2)), dma((2,)), dma((4,)), dma((4,)), dma((4,)), dma((2,)), dma((2,)), dma((4,)),
+            pltpu.VMEM((4 * LANES, 2 * LANES), f32),
         ],
         compiler_params=pltpu.CompilerParams(has_side_effects=True, collective_id=0, vmem_limit_bytes=limit), name="flow",
-    )(flow_state, jnp.asarray(band_matrix()), owner)
+    )(flow_state, owner)
     sent = pl.pallas_call(
         functools.partial(compact_kernel, n_tile),
         out_shape=shape((n_tile, rows, cap + 2 * LANES), f32),

time: 46.2 us -> 45.1 us (0.976)
  local copies, waits for them, and re-layouts: 3.41 us -> 2.37 us
    unnamed x9 -> x7, local copies, waits for them, and re-layouts: 3.41 us -> 2.37 us
where the time goes in v4:
time: 45.1 us; the launch traced here: 44.9 us
  Pallas kernels  42.5 us (94%)
  local copies, waits for them, and re-layouts  2.37 us (5%)
    pallas_call x1, Pallas kernels, body(): pl.pallas_call(functools.partial(flow_kernel, n_tile), out_shape=(shape(t...  23.9 us
    pallas_call x1, Pallas kernels, body(): pl.pallas_call(functools.partial(record_kernel, n_tile, chunks), out_shap...  13.1 us
    pallas_call x1, Pallas kernels, body(): pl.pallas_call(functools.partial(compact_kernel, n_tile), out_shape=shape...  5.47 us
    unnamed x7, local copies, waits for them, and re-layouts  2.37 us

profile of v4, /device:TPU:0, one launch (start us, length us, event | category | flops | bytes accessed | tf_op | source)
XLA Modules:
  0.0 44.9 jit_solution(4065979150339221717)
XLA Ops:
  0.0 0.0 copy-start
  0.0 0.9 %copy-done = f32[1,4,4,2048]{3,2,1,0:T(4,128)S(1)} copy-done((f32[1,4,4,2048]{3,2,1,0:T(4,128)S(1)}, f32[1,4,4,2048]{3,2,1,0:T(4,128)}, u32[]{:S(2)}) %copy-start) | copy-done | bytes 131096
  0.9 0.0 copy-start.1
  0.9 0.8 %copy-done.1 = s32[8192,1]{0,1:T(1,128)S(1)} copy-done((s32[8192,1]{0,1:T(1,128)S(1)}, s32[8192,1]{0,1:T(1,128)}, u32[]{:S(2)}) %copy-start.1) | copy-done | bytes 32792
  1.7 23.9 %flow.1 = (f32[4,4,2048]{2,1,0:T(4,128)S(1)}, f32[64,128]{1,0:T(8,128)S(1)}, s32[64,128]{1,0:T(8,128)S(1)}, s32[64,128]{1,0:T(8,128)S(1)}) custom-call(f32[1,4,4,2048]{3,2,1,0:T(4,128)S(1)} %copy-done, s32[64,128]{1,0:T(8,128)S(1)} %bitcast.3), custom_call_target="tpu_custom_call" | custom-call | tf_op jit(solution)/shard_map/flow/pallas_call | solution.py:467
  25.6 0.0 copy-start.2
  25.6 5.5 %compact.1.sent_ref = f32[8,4,2304]{2,1,0:T(4,128)S(1)} custom-call(s32[64,128]{1,0:T(8,128)S(1)} %get-tuple-element.9.base_ref, s32[64,128]{1,0:T(8,128)S(1)} %get-tuple-element.10.count_ref, f32[4,4,2048]{2,1,0:T(4,128)S(1)} %get-tuple-element.11.coeff_ref, f32[64,128]{1,0:T(8,128)S(1)} %get-tuple-element.12.place_ref), custom_call_target="tpu_custom_call" | custom-call | tf_op jit(solution)/shard_map/compact/pallas_call | solution.py:481
  31.0 0.0 copy-done.2
  31.0 13.1 %record.1 = f32[32,2048]{1,0:T(8,128)S(1)} custom-call(f32[8,4,2304]{2,1,0:T(4,128)S(1)} %compact.1.sent_ref, f32[32,32]{1,0:T(8,128)S(1)} %copy-done.2), custom_call_target="tpu_custom_call" | custom-call | tf_op jit(solution)/shard_map/record/pallas_call | solution.py:489
  44.2 0.7 %copy.5 = f32[1,1,32,2048]{3,2,1,0:T(8,128)} copy(f32[1,1,32,2048]{3,2,1,0:T(8,128)S(1)} %bitcast.2) | data formatting | bytes 524288
Async XLA Ops:
  0.0 0.9 %copy-start = (f32[1,4,4,2048]{3,2,1,0:T(4,128)S(1)}, f32[1,4,4,2048]{3,2,1,0:T(4,128)}, u32[]{:S(2)}) copy-start(f32[1,4,4,2048]{3,2,1,0:T(4,128)} %own_ref.1) | copy-start | bytes 393220
  0.9 0.8 %copy-start.1 = (s32[8192,1]{0,1:T(1,128)S(1)}, s32[8192,1]{0,1:T(1,128)}, u32[]{:S(2)}) copy-start(s32[8192,1]{0,1:T(1,128)} %param.4) | copy-start | bytes 98308
  25.6 5.5 %copy-start.2 = (f32[32,32]{1,0:T(8,128)S(1)}, f32[32,32]{1,0:T(8,128)}, u32[]{:S(2)}) copy-start(f32[32,32]{1,0:T(8,128)} %constant.2.clone.matrix_ref) | copy-start | bytes 12292
